TPU v7x, 128 devices: a whole 4x4x4 slice. The times are simulated.
128 devices in a mesh: dp: 8 (over x, core), tensor: 8 (over y_lo, z), section: 2 (over y_hi).
Axes of the slice: x: 4, y: 4 (y_hi: 2, y_lo: 2; y = y_hi * 2 + y_lo), z: 4, core: 2. Of those that a mesh axis runs over, the one named last changes fastest.
Arguments:
- patches: bfloat16 [32, 256, 1152], P(('dp', 'section'), 'tensor'), may hold values from -6 to 6
- teacher: int32 [32, 7], P(('dp', 'section')), may hold values from 0 to 255
- proj_w: bfloat16 [1152, 4096], P(None, ('dp', 'tensor', 'section')), may hold values from -0.1875 to 0.1875
- norm_gain: bfloat16 [4096], replicated, may hold values from 0.25 to 1.75
- wq: bfloat16 [4096, 4096], P(('dp', 'section'), 'tensor'), may hold values from -0.09375 to 0.09375
- wk: bfloat16 [4096, 4096], P(('dp', 'section'), 'tensor'), may hold values from -0.09375 to 0.09375
- wv: bfloat16 [4096, 4096], P(('dp', 'section'), 'tensor'), may hold values from -0.09375 to 0.09375
- wo: bfloat16 [4096, 4096], P('tensor', ('dp', 'section')), may hold values from -0.09375 to 0.09375
- start_row: bfloat16 [4096], replicated, may hold values from -6 to 6
- action_table: bfloat16 [256, 4096], replicated, may hold values from -6 to 6
- final_gain: bfloat16 [4096], replicated, may hold values from 0.25 to 1.75
- head_w: bfloat16 [4096, 256], replicated, may hold values from -0.25 to 0.25
Outputs:
- hidden_out: bfloat16 [32, 256, 4096], P(('dp', 'section'), 'tensor')
- loss: float32 [32, 7], P(('dp', 'section'))
All inputs are finite; a program needn't handle non-finite values.
Results may differ from a plain program's by a relative error of at most 0.0054.
Values may be sent and summed in bfloat16 or wider, within the bound.
No kernel may reach another device: no remote copies, remote signals or barrier semaphores. Data moves between devices by JAX's collectives and lax.ppermute only.
A program may use at most 128 MiB of HBM per device.

v0:
```python
import math
import jax
import jax.numpy as jnp
from jax import lax
from jax.sharding import PartitionSpec as P

D = 4096
HD = 128
V = 1152
P_SIZE = 256
BINS = 256
ADIM = 7
SLOTS = 8
eps = 1e-05


def joined_along(parts, dim):
    dims = list(parts.shape[1:])
    dims[dim] *= parts.shape[0]
    return jnp.moveaxis(parts, 0, dim).reshape(dims)


def from_everyone(shard, axis):
    devices = lax.axis_size(axis)
    return lax.all_to_all(
        jnp.broadcast_to(shard[None], (devices, *shard.shape)), axis, 0, 0, tiled=True
    )


def gathered_copies(shard, axis, dim):
    return joined_along(from_everyone(shard, axis), dim)


def side_by_side(arrays, axis, dim, along):
    widths = [a.shape[along] for a in arrays]
    both = jnp.concatenate(arrays, axis=along)
    filled = lax.all_gather(both, axis, axis=dim, tiled=True)
    return tuple(jnp.split(filled, [sum(widths[:k]) for k in range(1, len(widths))], axis=along))


def over_copies(shard, axis):
    everything = from_everyone(shard, axis)
    return jnp.sum(everything.astype(jnp.float32), axis=0)


def normalize(rows, gain):
    rows = rows.astype(jnp.float32)
    factor = lax.rsqrt(jnp.mean(rows * rows, axis=-1, keepdims=True) + eps)
    return rows * factor * gain.astype(jnp.float32)


def action_rows(teacher, start_row, action_table):
    frames = teacher.shape[0]
    onehot = (teacher[..., None] == jnp.arange(BINS, dtype=jnp.int32)).astype(jnp.bfloat16)
    looked = jnp.dot(onehot.reshape(-1, BINS), action_table, preferred_element_type=jnp.float32)
    looked = looked.astype(jnp.bfloat16).reshape(frames, ADIM, D)
    start = jnp.broadcast_to(start_row.reshape(1, 1, D), (frames, 1, D))
    return jnp.concatenate([start, looked], axis=1)


def embed(source_rows, proj_w):
    flat = source_rows.reshape(-1, V)
    result = jnp.dot(
        flat,
        lax.all_gather(proj_w, ("dp", "tensor", "section"), axis=1, tiled=True),
        preferred_element_type=jnp.float32,
    )
    return result.astype(jnp.bfloat16).reshape(source_rows.shape[0], source_rows.shape[1], D)


def on_device(
    patches, teacher, proj_w, norm_gain, wq, wk, wv, wo, start_row, action_table, final_gain, head_w
):
    frames = patches.shape[0]
    local_patches = patches.shape[1]
    length = P_SIZE + SLOTS
    all_patches = gathered_copies(patches, "tensor", 1)
    embedded_all = embed(all_patches, proj_w)
    embedded_own = lax.dynamic_slice_in_dim(
        embedded_all, lax.axis_index("tensor") * local_patches, local_patches, 1
    )
    actions = action_rows(teacher, start_row, action_table)
    stream = jnp.concatenate([embedded_all, actions], axis=1)
    normed = normalize(stream, norm_gain).astype(jnp.bfloat16).reshape(-1, D)
    local_width = wq.shape[1]
    full_query, full_key, full_value = side_by_side((wq, wk, wv), ("dp", "section"), 0, 1)
    projected = tuple(
        (
            jnp.dot(normed, weight, preferred_element_type=jnp.float32)
            for weight in (full_query, full_key, full_value)
        )
    )
    heads_local = local_width // HD
    queries, keys_all, values_all = [
        part.astype(jnp.bfloat16).reshape(frames, length, heads_local, HD) for part in projected
    ]
    inv_root = 1.0 / math.sqrt(HD)
    scores = (
        jnp.einsum("fqhd,fkhd->fhqk", queries, keys_all, preferred_element_type=jnp.float32)
        * inv_root
    )
    positions = jnp.arange(length, dtype=jnp.int32)
    causal = positions[:, None] >= positions[None, :]
    scores = jnp.where(causal[None, None], scores, -1e30)
    weights = jax.nn.softmax(scores, axis=-1).astype(jnp.bfloat16)
    mixed = jnp.einsum("fhqk,fkhd->fqhd", weights, values_all, preferred_element_type=jnp.float32)
    mixed = mixed.astype(jnp.bfloat16).reshape(frames, length, local_width)
    wo_rows = lax.all_gather(wo, ("dp", "section"), axis=1, tiled=True)
    patch_major = jnp.transpose(mixed[:, :P_SIZE], (1, 0, 2))
    product = jnp.dot(
        patch_major.reshape(-1, local_width), wo_rows, preferred_element_type=jnp.float32
    )
    own_rows = lax.psum_scatter(
        product.reshape(local_patches * lax.axis_size("tensor"), frames, D),
        "tensor",
        scatter_dimension=0,
        tiled=True,
    )
    patch_update = jnp.transpose(own_rows, (1, 0, 2))
    action_mixed = mixed[:, P_SIZE : P_SIZE + ADIM].reshape(-1, local_width)
    action_part = jnp.dot(action_mixed, wo_rows, preferred_element_type=jnp.float32).reshape(
        frames, ADIM, D
    )
    hidden_out = (embedded_own.astype(jnp.float32) + patch_update).astype(jnp.bfloat16)
    action_update = over_copies(action_part.astype(jnp.bfloat16), "tensor").astype(jnp.float32)
    acted = actions[:, :ADIM].astype(jnp.float32) + action_update
    final = normalize(acted, final_gain).astype(jnp.bfloat16).reshape(-1, D)
    logits = jnp.dot(final, head_w, preferred_element_type=jnp.float32).reshape(frames, ADIM, BINS)
    chosen = (teacher[..., None] == jnp.arange(BINS, dtype=jnp.int32)).astype(jnp.float32)
    picked = jnp.sum(logits * chosen, axis=-1)
    loss = jax.nn.logsumexp(logits, axis=-1) - picked
    return (hidden_out, loss)


def solution(mesh):
    return jax.shard_map(
        on_device,
        mesh=mesh,
        in_specs=(
            P(("dp", "section"), "tensor", None),
            P(("dp", "section"), None),
            P(None, ("dp", "tensor", "section")),
            P(),
            P(("dp", "section"), "tensor"),
            P(("dp", "section"), "tensor"),
            P(("dp", "section"), "tensor"),
            P("tensor", ("dp", "section")),
            P(),
            P(),
            P(),
            P(),
        ),
        out_specs=(P(("dp", "section"), "tensor", None), P(("dp", "section"), None)),
        check_vma=False,
    )
```

profile of v0, /device:TPU:1, one launch (start us, length us, event | category | flops | bytes accessed | tf_op | source)
XLA Modules:
  0.0 596.9 jit_solution(13776952633061691405)
XLA Ops:
  8.0 2.0 pad_maximum_fusion
  10.0 2.0 broadcast_in_dim.14
  12.1 6.9 %all-to-all-start = ((bf16[8,2,32,1152]{3,2,1,0:T(8,128)(2,1)}), bf16[8,2,32,1152]{3,2,1,0:T(8,128)(2,1)S(1)}, u32[]{:S(2)}, u32[]{:S(2)}) async-start(bf16[8,2,32,1152]{3,2,1,0:T(8,128)(2,1)} %broadcast_in_dim.14), calls=%async_computation | async-start | bytes 2359296 | tf_op jit(solution)/shard_map/all_to_all | solution.py:25
  20.3 15.0 %all-to-all-done = bf16[8,2,32,1152]{3,2,1,0:T(8,128)(2,1)S(1)} async-done(((bf16[8,2,32,1152]{3,2,1,0:T(8,128)(2,1)}), bf16[8,2,32,1152]{3,2,1,0:T(8,128)(2,1)S(1)}, u32[]{:S(2)}, u32[]{:S(2)}) %all-to-all-start) | async-done | bytes 1179680 | tf_op jit(solution)/shard_map/all_to_all | solution.py:25
  35.4 295.1 %all-gather.4.cloned.1.call-done = bf16[1152,4096]{0,1:T(8,128)(2,1)} async-done(((bf16[1152,32]{0,1:T(8,128)(2,1)}), bf16[1152,4096]{0,1:T(8,128)(2,1)}) %all-gather.4.cloned.1.call-update) | async-done | bytes 9437200 | tf_op jit(solution)/shard_map/all_gather | solution.py:65
  330.5 9.5 %convolution_convert_fusion = bf16[512,4096]{1,0:T(8,128)(2,1)S(1)} fusion(bf16[512,1152]{1,0:T(8,128)(2,1)S(1)} %bitcast.44, bf16[1152,4096]{0,1:T(8,128)(2,1)} %all-gather.4.cloned.1.call-done), kind=kOutput, calls=%fused_computation.5 | convolution fusion | flops 4833935360 | bytes 14811136 | tf_op jit(solution)/shard_map/dot_general | solution.py:63
  340.1 1.9 copy-done.2
  342.0 1.3 multiply_reduce_fusion
  343.4 2.8 maximum_convert_fusion
  346.2 3.6 fusion.2
  349.8 70.9 %all-gather.6.cloned.1.call-done = bf16[4096,1536]{1,0:T(8,128)(2,1)} async-done(((bf16[256,1536]{1,0:T(8,128)(2,1)}), bf16[4096,1536]{1,0:T(8,128)(2,1)}) %all-gather.6.cloned.1.call-update) | async-done | bytes 12582928 | tf_op jit(solution)/shard_map/all_gather | solution.py:37
  420.6 5.9 fusion.23
  426.7 5.9 fusion.26
  432.8 5.9 fusion.20
  439.5 1.3 fusion.40
  441.8 37.4 %all-gather.8.cloned.1.call-done = bf16[512,4096]{1,0:T(8,128)(2,1)} async-done(((bf16[512,256]{1,0:T(8,128)(2,1)}), bf16[512,4096]{1,0:T(8,128)(2,1)}) %all-gather.8.cloned.1.call-update) | async-done | bytes 4194320 | tf_op jit(solution)/shard_map/all_gather | solution.py:108
  479.2 7.8 %fusion.10 = f32[256,2,4096]{2,0,1:T(8,128)} fusion(bf16[512,4096]{1,0:T(8,128)(2,1)} %all-gather.8.cloned.1.call-done, bf16[2,264,512]{2,1,0:T(8,128)(2,1)S(1)} %bitcast.42), kind=kOutput, calls=%fused_computation.16 | convolution fusion | flops 2147483648 | bytes 13107200 | tf_op jit(solution)/shard_map/dot_general | solution.py:110
  487.0 2.9 convolution_convert_fusion.1
  490.0 1.8 broadcast_in_dim.22
  491.8 4.2 all-to-all-start.1
  496.2 25.0 %all-to-all-done.1 = bf16[8,2,7,4096]{3,1,2,0:T(2,128)(2,1)S(1)} async-done(((bf16[8,2,7,4096]{3,1,2,0:T(2,128)(2,1)}), bf16[8,2,7,4096]{3,1,2,0:T(2,128)(2,1)S(1)}, u32[]{:S(2)}, u32[]{:S(2)}) %all-to-all-start.1) | async-done | bytes 917536 | tf_op jit(solution)/shard_map/all_to_all | solution.py:25
  522.6 2.2 fusion.41
  525.6 62.5 %reduce-scatter.2.cloned.1.call-done = f32[32,2,4096]{2,0,1:T(8,128)} async-done(((f32[256,2,4096]{2,0,1:T(8,128)}), f32[32,2,4096]{2,0,1:T(8,128)}) %reduce-scatter.2.cloned.1.call-update) | async-done | bytes 1048592 | tf_op jit(solution)/shard_map/reduce_scatter | solution.py:113
  588.1 2.2 fusion.30
  (47 shorter events, 6.9 us)
Async XLA Ops:
  7.2 12.6 %copy-start = (bf16[256,4096]{1,0:T(8,128)(2,1)S(1)}, bf16[256,4096]{1,0:T(8,128)(2,1)}, u32[]{:S(2)}) copy-start(bf16[256,4096]{1,0:T(8,128)(2,1)} %param.21) | copy-start | bytes 6291460
  7.2 12.5 %copy-start.6 = (s32[2,7]{1,0:T(2,128)S(1)}, s32[2,7]{1,0:T(2,128)}, u32[]{:S(2)}) copy-start(s32[2,7]{1,0:T(2,128)} %param.13) | copy-start | bytes 172
  7.2 323.3 %all-gather.4.cloned.1.call-start = ((), (), s32[]{:S(2)}) async-start(), calls=%async_computation.3 | async-start | bytes 9510912 | tf_op jit(solution)/shard_map/all_gather | solution.py:65
  7.9 12.3 %copy-start.4 = (bf16[4096]{0:T(1024)(128)(2,1)S(1)}, bf16[4096]{0:T(1024)(128)(2,1)}, u32[]{:S(2)}) copy-start(bf16[4096]{0:T(1024)(128)(2,1)} %param.15) | copy-start | bytes 24580
  7.9 412.7 %all-gather.6.cloned.1.call-start = ((), (), s32[]{:S(2)}) async-start(), calls=%async_computation.4 | async-start | bytes 13369344 | tf_op jit(solution)/shard_map/all_gather | solution.py:37
  12.1 23.2 %all-to-all-start = ((bf16[8,2,32,1152]{3,2,1,0:T(8,128)(2,1)}), bf16[8,2,32,1152]{3,2,1,0:T(8,128)(2,1)S(1)}, u32[]{:S(2)}, u32[]{:S(2)}) async-start(bf16[8,2,32,1152]{3,2,1,0:T(8,128)(2,1)} %broadcast_in_dim.14), calls=%async_computation | async-start | bytes 2359296 | tf_op jit(solution)/shard_map/all_to_all | solution.py:25
  18.9 460.3 %all-gather.8.cloned.1.call-start = ((), (), s32[]{:S(2)}) async-start(), calls=%async_computation.5 | async-start | bytes 4456448 | tf_op jit(solution)/shard_map/all_gather | solution.py:108
  19.7 568.5 %reduce-scatter.2.cloned.1.call-start = ((), (), s32[]{:S(2)}) async-start(), calls=%async_computation.6 | async-start | bytes 9437184 | tf_op jit(solution)/shard_map/reduce_scatter | solution.py:113
  330.5 9.5 %copy-start.3 = (bf16[4096]{0:T(1024)(128)(2,1)S(1)}, bf16[4096]{0:T(1024)(128)(2,1)}, u32[]{:S(2)}) copy-start(bf16[4096]{0:T(1024)(128)(2,1)} %param.20) | copy-start | bytes 24580
  340.0 1.9 copy-start.2
  487.0 9.2 %copy-start.5 = (bf16[4096]{0:T(1024)(128)(2,1)S(1)}, bf16[4096]{0:T(1024)(128)(2,1)}, u32[]{:S(2)}) copy-start(bf16[4096]{0:T(1024)(128)(2,1)} %param.22) | copy-start | bytes 24580
  490.0 100.4 %copy-start.1 = (bf16[256,4096]{1,0:T(8,128)(2,1)S(1)}, bf16[256,4096]{1,0:T(8,128)(2,1)}, u32[]{:S(2)}) copy-start(bf16[256,4096]{1,0:T(8,128)(2,1)} %param.21) | copy-start | bytes 6291460
  491.8 29.3 %all-to-all-start.1 = ((bf16[8,2,7,4096]{3,1,2,0:T(2,128)(2,1)}), bf16[8,2,7,4096]{3,1,2,0:T(2,128)(2,1)S(1)}, u32[]{:S(2)}, u32[]{:S(2)}) async-start(bf16[8,2,7,4096]{3,1,2,0:T(2,128)(2,1)} %broadcast_in_dim.22), calls=%async_computation.2 | async-start | bytes 1835008 | tf_op jit(solution)/shard_map/all_to_all | solution.py:25
Sparse Core Ops, SparseCore 0:
  9.7 320.7 all-gather.3
  332.9 87.6 all-gather.5
  422.9 56.2 all-gather.7
  487.1 100.9 reduce-scatter.1
where the time goes:
time: 597 us
  waiting for transfers between devices  507 us (85%)
  matrix products  42.1 us (7%)
  other arithmetic  15.6 us (3%)
  between operations  14 us (2%)
  starting transfers between devices  11.2 us (2%)
  local copies, waits for them, and re-layouts  6.82 us (1%)
    all_gather x1, waiting for transfers between devices, embed(): lax.all_gather(proj_w, ('dp', 'tensor', 'section'), axis=1, tiled=True)  295 us
    all_gather x1, waiting for transfers between devices, side_by_side(): filled = lax.all_gather(both, axis, axis=dim, tiled=True)  70.9 us
    reduce_scatter x1, waiting for transfers between devices, on_device(): lax.psum_scatter(product.reshape(local_patches * lax.axis_size('tensor'),...  62.5 us
    all_to_all x2, waiting for transfers between devices, from_everyone(): lax.all_to_all(jnp.broadcast_to(shard[None], (devices, *shard.shape)), ax...  39.9 us
    all_gather x1, waiting for transfers between devices, on_device(): wo_rows = lax.all_gather(wo, ('dp', 'section'), axis=1, tiled=True)  37.4 us
    dot_general x3, matrix products, on_device(): jnp.dot(normed, weight, preferred_element_type=jnp.float32)  17.7 us
  transfers between devices with their start and end apart: 6, of which 6 were waited for; matrix products, arithmetic and copies ran while one was open for 9% of the time, Pallas kernels for 0%

commit v1 on v0

--- a/solution.py
+++ b/solution.py
@@ -3,6 +3,7 @@
 import jax.numpy as jnp
 from jax import lax
 from jax.sharding import PartitionSpec as P
+from jax.lax import all_to_all, axis_size
 
 D = 4096
 HD = 128
@@ -59,12 +60,17 @@
 
 
 def embed(source_rows, proj_w):
+
+    def _state_state(body):
+        z_new = jnp.stack([body for _ in range(axis_size(("dp", "tensor", "section")))])
+        wide_out = all_to_all(
+            z_new, split_axis=0, concat_axis=0, axis_name=("dp", "tensor", "section")
+        )
+        outer = jnp.concatenate(wide_out, axis=1)
+        return outer
+
     flat = source_rows.reshape(-1, V)
-    result = jnp.dot(
-        flat,
-        lax.all_gather(proj_w, ("dp", "tensor", "section"), axis=1, tiled=True),
-        preferred_element_type=jnp.float32,
-    )
+    result = jnp.dot(flat, _state_state(proj_w), preferred_element_type=jnp.float32)
     return result.astype(jnp.bfloat16).reshape(source_rows.shape[0], source_rows.shape[1], D)
 
 

time: 597 us -> 396 us (0.66)
  waiting for transfers between devices: 507 us -> 270 us
  blocking collectives: 0 us -> 26.3 us
    all_gather x1 -> x0, waiting for transfers between devices: 295 us -> none  [embed(): lax.all_gather(proj_w, ('dp', 'tensor', 'section'), axis=1, tiled=True)]
    all_to_all x0 -> x1, waiting for transfers between devices: none -> 138 us  [_state_state(): all_to_all(z_new, split_axis=0, concat_axis=0, axis_name=('dp', 'tensor',...]
    all_gather x1, waiting for transfers between devices: 70.9 us -> 2.31 us  [side_by_side(): filled = lax.all_gather(both, axis, axis=dim, tiled=True)]
    all_to_all x0 -> x1, blocking collectives: none -> 26.3 us  [from_everyone(): lax.all_to_all(jnp.broadcast_to(shard[None], (devices, *shard.shape)), ax...]
    all_to_all x2 -> x1, waiting for transfers between devices: 39.9 us -> 25 us  [from_everyone(): lax.all_to_all(jnp.broadcast_to(shard[None], (devices, *shard.shape)), ax...]
    all_to_all x0 -> x1, starting transfers between devices: none -> 12.5 us  [_state_state(): all_to_all(z_new, split_axis=0, concat_axis=0, axis_name=('dp', 'tensor',...]
    all_to_all x2 -> x1, starting transfers between devices: 11 us -> 4.17 us  [from_everyone(): lax.all_to_all(jnp.broadcast_to(shard[None], (devices, *shard.shape)), ax...]
  transfers between devices with their start and end apart: 6 -> 5, of which waited for: 6 -> 5; matrix products, arithmetic and copies ran while one was open for 9% -> 14% of each run, Pallas kernels for 0% -> 0%
where the time goes in v1:
time: 396 us
  waiting for transfers between devices  270 us (68%)
  matrix products  42.2 us (11%)
  blocking collectives  26.3 us (7%)
  starting transfers between devices  16.8 us (4%)
  other arithmetic  15.9 us (4%)
  between operations  14 us (4%)
  local copies, waits for them, and re-layouts  10.2 us (3%)
    all_to_all x1, waiting for transfers between devices, _state_state(): all_to_all(z_new, split_axis=0, concat_axis=0, axis_name=('dp', 'tensor',...  138 us
    reduce_scatter x1, waiting for transfers between devices, on_device(): lax.psum_scatter(product.reshape(local_patches * lax.axis_size('tensor'),...  62.5 us
    all_gather x1, waiting for transfers between devices, on_device(): wo_rows = lax.all_gather(wo, ('dp', 'section'), axis=1, tiled=True)  42.2 us
    all_to_all x1, blocking collectives, from_everyone(): lax.all_to_all(jnp.broadcast_to(shard[None], (devices, *shard.shape)), ax...  26.3 us
    all_to_all x1, waiting for transfers between devices, from_everyone(): lax.all_to_all(jnp.broadcast_to(shard[None], (devices, *shard.shape)), ax...  25 us
    dot_general x3, matrix products, on_device(): jnp.dot(normed, weight, preferred_element_type=jnp.float32)  17.9 us
    all_to_all x1, starting transfers between devices, _state_state(): all_to_all(z_new, split_axis=0, concat_axis=0, axis_name=('dp', 'tensor',...  12.5 us
    dot_general x1, matrix products, embed(): jnp.dot(flat, _state_state(proj_w), preferred_element_type=jnp.float32)  9.53 us
  transfers between devices with their start and end apart: 5, of which 5 were waited for; matrix products, arithmetic and copies ran while one was open for 14% of the time, Pallas kernels for 0%

profile of v1, /device:TPU:1, one launch (start us, length us, event | category | flops | bytes accessed | tf_op | source)
XLA Modules:
  0.0 395.8 jit_solution(8170413930369280385)
XLA Ops:
  7.2 2.2 pad_maximum_fusion
  10.5 26.3 %all_to_all.15 = bf16[8,2,32,1152]{3,2,1,0:T(8,128)(2,1)S(1)} all-to-all(bf16[8,2,32,1152]{3,2,1,0:T(8,128)(2,1)S(1)} %broadcast_in_dim.14), channel_id=1, replica_groups=mesh['dp'=8,'tensor'=8,'section'=2] {'tensor'}, dimensions={0} | all-to-all | bytes 2359296 | tf_op jit(solution)/shard_map/all_to_all | solution.py:26
  36.8 4.3 %stack.2 = bf16[128,1152,32]{1,2,0:T(8,128)(2,1)} broadcast(bf16[1152,32]{0,1:T(8,128)(2,1)S(1)} %copy-done.3), dimensions={1,2} | broadcast | bytes 9510912 | tf_op jit(solution)/shard_map/stack | solution.py:65
  41.1 12.5 %all-to-all-start.1 = ((bf16[128,1152,32]{1,2,0:T(8,128)(2,1)}), bf16[128,1152,32]{1,2,0:T(8,128)(2,1)}, u32[]{:S(2)}, u32[]{:S(2)}) async-start(bf16[128,1152,32]{1,2,0:T(8,128)(2,1)} %stack.2), calls=%async_computation.1 | async-start | bytes 18874368 | tf_op jit(solution)/shard_map/all_to_all | solution.py:66
  55.1 137.8 %all-to-all-done.1 = bf16[128,1152,32]{1,2,0:T(8,128)(2,1)} async-done(((bf16[128,1152,32]{1,2,0:T(8,128)(2,1)}), bf16[128,1152,32]{1,2,0:T(8,128)(2,1)}, u32[]{:S(2)}, u32[]{:S(2)}) %all-to-all-start.1) | async-done | bytes 9437216 | tf_op jit(solution)/shard_map/all_to_all | solution.py:66
  192.8 9.5 %convolution_convert_fusion = bf16[512,4096]{1,0:T(8,128)(2,1)S(1)} fusion(bf16[512,1152]{1,0:T(8,128)(2,1)S(1)} %bitcast.47, bf16[1152,4096]{0,1:T(8,128)(2,1)} %bitcast.3), kind=kOutput, calls=%fused_computation.5 | convolution fusion | flops 4833935360 | bytes 14811136 | tf_op jit(solution)/shard_map/dot_general | solution.py:73
  202.4 1.9 copy-done.2
  204.3 1.3 multiply_reduce_fusion
  205.7 2.9 maximum_convert_fusion
  208.7 3.6 fusion.2
  212.3 2.3 all-gather.3.cloned.1.call-done
  214.6 5.9 %fusion.23 = bf16[528,512]{1,0:T(8,128)(2,1)S(1)} fusion(bf16[528,4096]{1,0:T(8,128)(2,1)} %fusion.2, bf16[4096,1536]{1,0:T(8,128)(2,1)} %all-gather.3.cloned.1.call-done), kind=kOutput, calls=%fused_computation.31 | convolution fusion | flops 2214862848 | bytes 9060352 | tf_op jit(solution)/shard_map/dot_general | solution.py:95
  220.6 5.9 %fusion.26 = bf16[528,512]{1,0:T(8,128)(2,1)S(1)} fusion(bf16[528,4096]{1,0:T(8,128)(2,1)} %fusion.2, bf16[4096,1536]{1,0:T(8,128)(2,1)} %all-gather.3.cloned.1.call-done), kind=kOutput, calls=%fused_computation.32 | convolution fusion | flops 2214862848 | bytes 9060352 | tf_op jit(solution)/shard_map/dot_general | solution.py:95
  226.7 6.1 %fusion.20 = bf16[528,512]{1,0:T(8,128)(2,1)S(1)} fusion(bf16[528,4096]{1,0:T(8,128)(2,1)} %fusion.2, bf16[4096,1536]{1,0:T(8,128)(2,1)} %all-gather.3.cloned.1.call-done), kind=kOutput, calls=%fused_computation.30 | convolution fusion | flops 2214862848 | bytes 9060352 | tf_op jit(solution)/shard_map/dot_general | solution.py:95
  233.6 1.3 fusion.40
  235.9 42.2 %all-gather.5.cloned.1.call-done = bf16[512,4096]{1,0:T(8,128)(2,1)} async-done(((bf16[512,256]{1,0:T(8,128)(2,1)}), bf16[512,4096]{1,0:T(8,128)(2,1)}) %all-gather.5.cloned.1.call-update) | async-done | bytes 4194320 | tf_op jit(solution)/shard_map/all_gather | solution.py:114
  278.1 7.8 %fusion.10 = f32[256,2,4096]{2,0,1:T(8,128)} fusion(bf16[512,4096]{1,0:T(8,128)(2,1)} %all-gather.5.cloned.1.call-done, bf16[2,264,512]{2,1,0:T(8,128)(2,1)S(1)} %bitcast.45), kind=kOutput, calls=%fused_computation.16 | convolution fusion | flops 2147483648 | bytes 13107200 | tf_op jit(solution)/shard_map/dot_general | solution.py:116
  285.9 2.9 convolution_convert_fusion.1
  288.9 1.8 broadcast_in_dim.22
  290.8 4.2 %all-to-all-start.2 = ((bf16[8,2,7,4096]{3,1,2,0:T(2,128)(2,1)}), bf16[8,2,7,4096]{3,1,2,0:T(2,128)(2,1)S(1)}, u32[]{:S(2)}, u32[]{:S(2)}) async-start(bf16[8,2,7,4096]{3,1,2,0:T(2,128)(2,1)} %broadcast_in_dim.22), calls=%async_computation.3 | async-start | bytes 1835008 | tf_op jit(solution)/shard_map/all_to_all | solution.py:26
  295.1 25.0 %all-to-all-done.2 = bf16[8,2,7,4096]{3,1,2,0:T(2,128)(2,1)S(1)} async-done(((bf16[8,2,7,4096]{3,1,2,0:T(2,128)(2,1)}), bf16[8,2,7,4096]{3,1,2,0:T(2,128)(2,1)S(1)}, u32[]{:S(2)}, u32[]{:S(2)}) %all-to-all-start.2) | async-done | bytes 917536 | tf_op jit(solution)/shard_map/all_to_all | solution.py:26
  321.5 2.2 fusion.41
  324.5 62.5 %reduce-scatter.2.cloned.1.call-done = f32[32,2,4096]{2,0,1:T(8,128)} async-done(((f32[256,2,4096]{2,0,1:T(8,128)}), f32[32,2,4096]{2,0,1:T(8,128)}) %reduce-scatter.2.cloned.1.call-update) | async-done | bytes 1048592 | tf_op jit(solution)/shard_map/reduce_scatter | solution.py:119
  387.0 2.2 fusion.30
  (48 shorter events, 7.2 us)
Async XLA Ops:
  7.2 47.3 %copy-start = (bf16[256,4096]{1,0:T(8,128)(2,1)S(1)}, bf16[256,4096]{1,0:T(8,128)(2,1)}, u32[]{:S(2)}) copy-start(bf16[256,4096]{1,0:T(8,128)(2,1)} %param.21) | copy-start | bytes 6291460
  7.2 29.6 %copy-start.3 = (bf16[1152,32]{0,1:T(8,128)(2,1)S(1)}, bf16[1152,32]{0,1:T(8,128)(2,1)}, u32[]{:S(2)}) copy-start(bf16[1152,32]{0,1:T(8,128)(2,1)} %param.14) | copy-start | bytes 221188
  7.2 207.4 %all-gather.3.cloned.1.call-start = ((), (), s32[]{:S(2)}) async-start(), calls=%async_computation.4 | async-start | bytes 13369344 | tf_op jit(solution)/shard_map/all_gather | solution.py:38
  41.1 13.3 %copy-start.7 = (s32[2,7]{1,0:T(2,128)S(1)}, s32[2,7]{1,0:T(2,128)}, u32[]{:S(2)}) copy-start(s32[2,7]{1,0:T(2,128)} %param.13) | copy-start | bytes 172
  41.1 13.8 %copy-start.5 = (bf16[4096]{0:T(1024)(128)(2,1)S(1)}, bf16[4096]{0:T(1024)(128)(2,1)}, u32[]{:S(2)}) copy-start(bf16[4096]{0:T(1024)(128)(2,1)} %param.15) | copy-start | bytes 24580
  41.1 151.8 %all-to-all-start.1 = ((bf16[128,1152,32]{1,2,0:T(8,128)(2,1)}), bf16[128,1152,32]{1,2,0:T(8,128)(2,1)}, u32[]{:S(2)}, u32[]{:S(2)}) async-start(bf16[128,1152,32]{1,2,0:T(8,128)(2,1)} %stack.2), calls=%async_computation.1 | async-start | bytes 18874368 | tf_op jit(solution)/shard_map/all_to_all | solution.py:66
  53.6 224.6 %all-gather.5.cloned.1.call-start = ((), (), s32[]{:S(2)}) async-start(), calls=%async_computation.5 | async-start | bytes 4456448 | tf_op jit(solution)/shard_map/all_gather | solution.py:114
  54.3 332.7 %reduce-scatter.2.cloned.1.call-start = ((), (), s32[]{:S(2)}) async-start(), calls=%async_computation.6 | async-start | bytes 9437184 | tf_op jit(solution)/shard_map/reduce_scatter | solution.py:119
  192.8 9.6 %copy-start.4 = (bf16[4096]{0:T(1024)(128)(2,1)S(1)}, bf16[4096]{0:T(1024)(128)(2,1)}, u32[]{:S(2)}) copy-start(bf16[4096]{0:T(1024)(128)(2,1)} %param.20) | copy-start | bytes 24580
  202.4 1.9 copy-start.2
  285.9 9.2 %copy-start.6 = (bf16[4096]{0:T(1024)(128)(2,1)S(1)}, bf16[4096]{0:T(1024)(128)(2,1)}, u32[]{:S(2)}) copy-start(bf16[4096]{0:T(1024)(128)(2,1)} %param.22) | copy-start | bytes 24580
  288.9 100.4 %copy-start.1 = (bf16[256,4096]{1,0:T(8,128)(2,1)S(1)}, bf16[256,4096]{1,0:T(8,128)(2,1)}, u32[]{:S(2)}) copy-start(bf16[256,4096]{1,0:T(8,128)(2,1)} %param.21) | copy-start | bytes 6291460
  290.8 29.3 %all-to-all-start.2 = ((bf16[8,2,7,4096]{3,1,2,0:T(2,128)(2,1)}), bf16[8,2,7,4096]{3,1,2,0:T(2,128)(2,1)S(1)}, u32[]{:S(2)}, u32[]{:S(2)}) async-start(bf16[8,2,7,4096]{3,1,2,0:T(2,128)(2,1)} %broadcast_in_dim.22), calls=%async_computation.3 | async-start | bytes 1835008 | tf_op jit(solution)/shard_map/all_to_all | solution.py:26
Sparse Core Ops, SparseCore 0:
  10.4 204.1 all-gather.2
  216.9 61.2 all-gather.4
  286.0 100.9 reduce-scatter.1
